TPU v7x, 32 devices: a whole 2x2x4 slice. The times are simulated.
32 devices in a mesh: sfc: 8 (over z, core), lev: 4 (over y, x).
Axes of the slice: x: 2, y: 2, z: 4, core: 2. Of those that a mesh axis runs over, the one named last changes fastest.
Arguments:
- tracer_old: float32 [4, 10, 16, 3072], P('lev', None, None, 'sfc'), may hold values from 0.1 to 2
- air_old: float32 [4, 16, 3072], P('lev', None, 'sfc'), may hold values from 0.3 to 20, as said below
- air_new: float32 [4, 16, 3072], P('lev', None, 'sfc'), may hold values from 0.4 to 20, as said below
- dep_coord: float32 [2, 4, 16, 3072], P(None, 'lev', None, 'sfc'), may hold values from -1 to 1
- dep_slot: int32 [4, 16, 3072], P('lev', None, 'sfc'), may hold values from 0 to 639
- fetch_list: int32 [8, 2, 128], P('sfc'), may hold values from 0 to 383, as said below
Outputs:
- tracer_new: float32 [4, 10, 16, 3072], P('lev', None, None, 'sfc')
Inputs may be any that keep to these rules, and one draw needn't show every extreme that they name: `fetch_list`: side 0 holds distinct indices in [128, 384); side 1 holds distinct indices in [0, 256). `air_old`: positive. `air_new`: positive.
All inputs are finite; a program needn't handle non-finite values.
Results may differ from a plain program's by a relative error of at most 0.0003.
Values sent between devices are 32-bit elements; how exact they have to be, the bound alone decides.
A program may use at most 64 MiB of HBM per device.

v0:
```python
import functools

import jax
import jax.numpy as jnp
from jax import lax
from jax.experimental import pallas as pl
from jax.experimental.pallas import tpu as pltpu
from jax.sharding import PartitionSpec as P

BAND = 256
LANES = 128
SUB = 8
NODES = (-1.0, -0.4472135954999579, 0.4472135954999579, 1.0)
MESH = pl.DeviceIdType.MESH


def basis(coord):
    terms = []
    for first in range(4):
        term = None
        scale = 1.0
        for other in range(4):
            if other != first:
                factor = coord - NODES[other]
                term = factor if term is None else term * factor
                scale = scale / (NODES[first] - NODES[other])
        terms.append(term * scale)
    return terms


def lookup(values, index):
    return jnp.take_along_axis(values, index, axis=1, mode="promise_in_bounds")


def wide(row):
    return jnp.broadcast_to(row, (SUB, LANES))


def kernel(
    sizes, tr, air_old, air_new, coord, slot, fetch, out,
    natural, stage, table, halo, side, along_a, along_b, mixed_a, mixed_b, places, masses, masses_old, coords, wanted,
    kept, begun, message, heard, load_sem, halo_send, halo_recv, sum_send, sum_recv, ready,
):
    n_sfc, n_lev = sizes
    n_all = n_sfc * n_lev
    points = slot.shape[0]
    tracers, _, e_dev = tr.shape
    groups = e_dev // LANES
    row_groups = tracers * points // SUB
    halves = points // SUB
    flat = tracers * SUB
    mains = points
    rests = row_groups - mains
    band_groups = BAND // LANES
    me_s, me_l = lax.axis_index("sfc"), lax.axis_index("lev")
    me = me_s * n_lev + me_l

    def spot(distance):
        other = lax.rem(me + distance, n_all)
        return (lax.div(other, n_lev), lax.rem(other, n_lev))

    barrier = pltpu.get_barrier_semaphore()

    def greet_s(distance, carry):
        pl.semaphore_signal(
            barrier, inc=1, device_id=(lax.rem(me_s + distance, n_sfc), me_l), device_id_type=MESH
        )
        return carry

    def greet_l(sem, distance, carry):
        pl.semaphore_signal(
            sem, inc=1, device_id=(me_s, lax.rem(me_l + distance, n_lev)), device_id_type=MESH
        )
        return carry

    lax.fori_loop(1, n_sfc, greet_s, 0)
    lax.fori_loop(1, n_lev, functools.partial(greet_l, barrier), 0)

    def cols(group):
        return pl.ds(group * LANES, LANES)

    loads = []

    def load(source, target):
        copy = pltpu.make_async_copy(source, target, load_sem.at[len(loads)])
        copy.start()
        loads.append(copy)

    for g in range(groups):
        for h in range(halves):
            load(tr.at[:, pl.ds(h * SUB, SUB), cols(g)], natural.at[g, h])
        load(slot.at[:, cols(g)], places.at[g])
        load(coord.at[:, :, cols(g)], coords.at[g])
    for g in range(groups):
        load(air_old.at[:, cols(g)], masses_old.at[g])
        load(air_new.at[:, cols(g)], masses.at[g])
    load(fetch, wanted)

    def picked_rows(group):
        if group < mains:
            return pl.ds(group % SUB, SUB, stride=SUB)
        return pl.ds(SUB * SUB + (group - mains) % 2, SUB, stride=2)

    def half_of(h):
        return list(range(SUB * h, SUB * h + SUB)) + [mains + 2 * h, mains + 2 * h + 1]

    def prepare():
        for copy in loads:
            copy.wait()
        for h in range(halves):
            for g in range(groups):
                block = natural.at[g, h].reshape(flat, LANES)
                for r in half_of(h):
                    table[g, pl.ds(r * SUB, SUB), :] = block[picked_rows(r), :]
        for g in range(groups):
            for i, term in enumerate(basis(coords[g, 0])):
                along_a[i, g] = term
                for s in (0, 1, 4, 5):
                    mixed_a[i // 2, g, pl.ds(s + 2 * (i % 2), points, stride=SUB), :] = term
            for m, term in enumerate(basis(coords[g, 1])):
                along_b[m, g] = term
                for s in (0, 2, 4, 6):
                    mixed_b[m % 2, g, pl.ds(s + m // 2, points, stride=SUB), :] = term

    def half_shares(point, n, e, h):
        terms_b = [wide(along_b[m, e, pl.ds(n, 1), :]) for m in range(4)]
        interp = low = high = None
        for i in (2 * h, 2 * h + 1):
            inner = None
            for m in range(4):
                value = point(4 * i + m)
                low = value if low is None else jnp.minimum(low, value)
                high = value if high is None else jnp.maximum(high, value)
                scaled = terms_b[m] * value
                inner = scaled if inner is None else inner + scaled
            inner = inner * wide(along_a[i, e, pl.ds(n, 1), :])
            interp = inner if interp is None else interp + inner
        rest = low_rest = high_rest = None
        for q in range(2):
            value = point(mains + 2 * h + q)
            low_rest = value if low_rest is None else jnp.minimum(low_rest, value)
            high_rest = value if high_rest is None else jnp.maximum(high_rest, value)
            scaled = mixed_b[q, e, pl.ds(n * SUB, SUB), :] * value
            rest = scaled if rest is None else rest + scaled
        rest = rest * mixed_a[h, e, pl.ds(n * SUB, SUB), :]
        return (interp, low, high), (rest, low_rest, high_rest)

    def joined(one, two):
        return [
            (a[0] + b[0], jnp.minimum(a[1], b[1]), jnp.maximum(a[2], b[2])) for a, b in zip(one, two)
        ]

    def shares(point, n, e):
        return joined(half_shares(point, n, e, 0), half_shares(point, n, e, 1))

    def own(n, carry):
        for e in range(groups):
            row = wide(places[e, pl.ds(n, 1), :])
            low_index, high_index = row & (LANES - 1), row >> 7
            above = [high_index == g for g in range(1, groups)]

            def point(r):
                here = pl.ds(r * SUB, SUB)
                value = lookup(table[0, here, :], low_index)
                for g in range(1, groups):
                    value = jnp.where(above[g - 1], lookup(table[g, here, :], low_index), value)
                return value

            for b, kinds in enumerate(shares(point, n, e)):
                for q, kind in enumerate(kinds):
                    kept[b, q, n, :, cols(e)] = kind
        return carry

    def receive(k, h):
        for g in range(band_groups):
            pltpu.make_async_copy(halo.at[k, g, h], halo.at[k, g, h], halo_recv.at[k, g, h]).wait()
        index = wide(wanted[pl.ds(k, 1), :]) - jnp.where(k == 0, e_dev - BAND, 0)
        index_low, index_high = index & (LANES - 1), index >> 7
        blocks = [halo.at[k, g, h].reshape(flat, LANES) for g in range(band_groups)]
        for r in half_of(h):
            value = lookup(blocks[0][picked_rows(r), :], index_low)
            for g in range(1, band_groups):
                value = jnp.where(
                    index_high == g, lookup(blocks[g][picked_rows(r), :], index_low), value
                )
            side[pl.ds(r * SUB, SUB), :] = value

    def chosen(k, n, e):
        row = wide(places[e, pl.ds(n, 1), :])
        low_index, mine = row & (LANES - 1), (row >> 7) == groups + k

        def point(r):
            return lookup(side[pl.ds(r * SUB, SUB), :], low_index)

        def merge(found):
            return [
                [jnp.where(mine, kind, kept[b, q, n, :, cols(e)]) for q, kind in enumerate(kinds)]
                for b, kinds in enumerate(found)
            ]

        return point, merge

    def near_pass(k, n, carry):
        for e in range(groups):
            point, merge = chosen(k, n, e)
            for b, kinds in enumerate(merge(shares(point, n, e))):
                for q, kind in enumerate(kinds):
                    kept[b, q, n, :, cols(e)] = kind
        return carry

    def begin_pass(k, n, carry):
        for e in range(groups):
            point, _ = chosen(k, n, e)
            for b, kinds in enumerate(half_shares(point, n, e, 0)):
                for q, kind in enumerate(kinds):
                    begun[b, q, n, :, cols(e)] = kind
        return carry

    def far_pass(k, n, carry):
        sums = list(carry)
        for e in range(groups):
            mass = wide(masses[e, pl.ds(n, 1), :])
            point, merge = chosen(k, n, e)
            first = [[begun[b, q, n, :, cols(e)] for q in range(3)] for b in range(2)]
            found = joined(first, half_shares(point, n, e, 1))
            for b, (value, least, most) in enumerate(merge(found)):
                for shift in (1, 2) if b else ():
                    value = value + pltpu.roll(value, SUB - shift, 0)
                    least = jnp.minimum(least, pltpu.roll(least, SUB - shift, 0))
                    most = jnp.maximum(most, pltpu.roll(most, SUB - shift, 0))
                clipped = jnp.minimum(jnp.maximum(value, least), most)
                for q, kind in enumerate((clipped, most - clipped, clipped - least)):
                    kept[b, q, n, :, cols(e)] = kind
                    sums[3 * b + q] = sums[3 * b + q] + mass * kind
        return tuple(sums)

    early = points // 2
    prepare()
    lax.fori_loop(0, early, own, 0, unroll=4)
    pl.semaphore_wait(barrier, n_sfc + n_lev - 2)
    right = (lax.rem(me_s + 1, n_sfc), me_l)
    left = (lax.rem(me_s + n_sfc - 1, n_sfc), me_l)
    sends = []
    for h in range(halves):
        for k, (target, start) in enumerate(((right, e_dev - BAND), (left, 0))):
            for g in range(band_groups):
                send = pltpu.make_async_remote_copy(
                    src_ref=tr.at[:, pl.ds(h * SUB, SUB), pl.ds(start + g * LANES, LANES)],
                    dst_ref=halo.at[k, g, h],
                    send_sem=halo_send.at[k, g, h],
                    recv_sem=halo_recv.at[k, g, h],
                    device_id=target,
                    device_id_type=MESH,
                )
                send.start()
                sends.append(send)
    lax.fori_loop(1, n_lev, functools.partial(greet_l, ready), 0)
    lax.fori_loop(early, points, own, 0, unroll=4)

    lane = lax.broadcasted_iota(jnp.int32, (SUB, LANES), 1)
    row = lax.broadcasted_iota(jnp.int32, (SUB, LANES), 0)
    old_main = jnp.zeros((SUB, LANES), jnp.float32)
    for j in range(mains):
        for g in range(groups):
            old_main += table[g, pl.ds(j * SUB, SUB), :] * wide(masses_old[g, pl.ds(j, 1), :])
    packed = jnp.where(lane == row, jnp.sum(old_main, axis=1, keepdims=True), 0.0)
    for t in range(SUB, tracers):
        product = sum(
            natural[g, h, t] * masses_old[g, pl.ds(h * SUB, SUB), :]
            for g in range(groups)
            for h in range(halves)
        )
        total = jnp.sum(jnp.sum(product, axis=1, keepdims=True), axis=0, keepdims=True)
        at = 4 * (t - SUB)
        packed = jnp.where((lane == 4 * SUB + row) & (row == at), total, packed)

    far = lax.rem(me_s, 2)
    near = 1 - far
    for h in range(halves):
        receive(near, h)
    lax.fori_loop(0, points, functools.partial(near_pass, near), 0, unroll=4)
    receive(far, 0)
    lax.fori_loop(0, points, functools.partial(begin_pass, far), 0, unroll=4)
    receive(far, 1)
    zero = jnp.zeros((SUB, LANES), jnp.float32)
    sums = lax.fori_loop(0, points, functools.partial(far_pass, far), (zero,) * 6, unroll=4)

    for b in range(2):
        for q in range(3):
            total = jnp.sum(sums[3 * b + q], axis=1, keepdims=True)
            packed = jnp.where(lane == (4 * b + q + 1) * SUB + row, total, packed)
    packed = jnp.sum(packed, axis=0, keepdims=True)
    message[...] = packed

    pl.semaphore_wait(ready, n_lev - 1)

    def tell(distance, carry):
        pltpu.make_async_remote_copy(
            src_ref=message,
            dst_ref=heard.at[distance - 1],
            send_sem=sum_send,
            recv_sem=sum_recv,
            device_id=spot(distance),
            device_id_type=MESH,
        ).start()
        return carry

    lax.fori_loop(1, n_all, tell, 0)
    pltpu.make_async_copy(heard, heard, sum_recv).wait()
    total = packed
    for k in range(n_all - 1) if n_all <= 64 else ():
        total = total + heard[k]
    if n_all > 64:
        total = lax.fori_loop(0, n_all - 1, lambda k, acc: acc + heard[k], total)

    old, clip, up, down = [
        wide(total) if q == 0 else pltpu.roll(wide(total), LANES - q * SUB, 1) for q in range(4)
    ]
    shortfall = old - clip
    raised = jnp.where(shortfall >= 0, shortfall / up, 0.0)
    lowered = jnp.where(shortfall >= 0, 0.0, shortfall / down)
    gains = []
    for b in range(2):
        pair = []
        for gain in (raised, lowered):
            column = jnp.where(lane == 4 * b * SUB + row, gain, 0.0)
            pair.append(jnp.broadcast_to(jnp.sum(column, axis=1, keepdims=True), (SUB, LANES)))
        gains.append(pair)

    def fix(n, carry):
        for e in range(groups):
            done = []
            for b in range(2):
                clipped, up, down = [kept[b, q, n, :, cols(e)] for q in range(3)]
                done.append(clipped + (gains[b][0] * up + gains[b][1] * down))
            stage[e, pl.ds(n, SUB, stride=points), :] = done[0]
            for t in range(SUB, tracers):
                at = 4 * (t - SUB)
                stage[e, pl.ds(t * points + n, 1), :] = done[1][at : at + 1]
        return carry

    lax.fori_loop(0, points, fix, 0, unroll=2)
    for g in range(groups):
        out[:, cols(g)] = stage[g]
    for send in sends:
        send.wait_send()
    pltpu.make_async_copy(heard, heard, sum_send).wait()


def solution(mesh):
    sizes = (mesh.shape["sfc"], mesh.shape["lev"])
    n_all = sizes[0] * sizes[1]

    def on_device(tracer_old, air_old, air_new, dep_coord, dep_slot, fetch_list):
        levels, tracers, points, e_dev = tracer_old.shape
        cap = fetch_list.shape[2]
        assert levels == 1 and cap == LANES and tracers == SUB + 2 and points == 16
        rows = tracers * points
        groups, halves = e_dev // LANES, points // SUB
        vmem = pl.BlockSpec(memory_space=pltpu.VMEM)
        result = pl.pallas_call(
            functools.partial(kernel, sizes),
            out_shape=pltpu.VMEM((rows, e_dev), jnp.float32),
            in_specs=[pl.BlockSpec(memory_space=pl.ANY)] * 6,
            out_specs=vmem,
            scratch_shapes=[
                pltpu.VMEM((groups, halves, tracers, SUB, LANES), jnp.float32),
                pltpu.VMEM((groups, rows, LANES), jnp.float32),
                pltpu.VMEM((groups, rows, LANES), jnp.float32),
                pltpu.VMEM((2, BAND // LANES, halves, tracers, SUB, LANES), jnp.float32),
                pltpu.VMEM((rows, LANES), jnp.float32),
                pltpu.VMEM((4, groups, points, LANES), jnp.float32),
                pltpu.VMEM((4, groups, points, LANES), jnp.float32),
                pltpu.VMEM((2, groups, points * SUB, LANES), jnp.float32),
                pltpu.VMEM((2, groups, points * SUB, LANES), jnp.float32),
                pltpu.VMEM((groups, points, LANES), jnp.int32),
                pltpu.VMEM((groups, points, LANES), jnp.float32),
                pltpu.VMEM((groups, points, LANES), jnp.float32),
                pltpu.VMEM((groups, 2, points, LANES), jnp.float32),
                pltpu.VMEM((2, cap), jnp.int32),
                pltpu.VMEM((2, 3, points, SUB, e_dev), jnp.float32),
                pltpu.VMEM((2, 3, points, SUB, e_dev), jnp.float32),
                pltpu.VMEM((1, LANES), jnp.float32),
                pltpu.VMEM((n_all - 1, 1, LANES), jnp.float32),
                pltpu.SemaphoreType.DMA(((4 + halves) * groups + 1,)),
                pltpu.SemaphoreType.DMA((2, BAND // LANES, halves)),
                pltpu.SemaphoreType.DMA((2, BAND // LANES, halves)),
                pltpu.SemaphoreType.DMA,
                pltpu.SemaphoreType.DMA,
                pltpu.SemaphoreType.REGULAR,
            ],
            compiler_params=pltpu.CompilerParams(collective_id=0, has_side_effects=True),
            name="transport",
        )(
            tracer_old.reshape(tracers, points, e_dev),
            air_old.reshape(points, e_dev),
            air_new.reshape(points, e_dev),
            dep_coord.reshape(2, points, e_dev),
            dep_slot.reshape(points, e_dev),
            fetch_list.reshape(2, cap),
        )
        return result.reshape(levels, tracers, points, e_dev)

    return jax.shard_map(
        on_device,
        mesh=mesh,
        in_specs=(
            P("lev", None, None, "sfc"),
            P("lev", None, "sfc"),
            P("lev", None, "sfc"),
            P(None, "lev", None, "sfc"),
            P("lev", None, "sfc"),
            P("sfc", None, None),
        ),
        out_specs=P("lev", None, None, "sfc"),
        check_vma=False,
    )
```

profile of v0, /device:TPU:0, one launch (start us, length us, event | category | flops | bytes accessed | tf_op | source)
XLA Modules:
  0.0 18.8 jit_solution(16962087986740851462)
XLA Ops:
  0.0 18.1 %transport.1 = f32[160,384]{1,0:T(8,128)S(1)} custom-call(f32[10,16,384]{2,1,0:T(8,128)} %bitcast.8, f32[16,384]{1,0:T(8,128)} %bitcast.10, f32[16,384]{1,0:T(8,128)} %bitcast.11, f32[2,16,384]{2,1,0:T(8,128)} %bitcast.9, s32[16,384]{1,0:T(8,128)} %bitcast.12, s32[2,128]{1,0:T(2,128)} %bitcast.13), custom_call_target="tpu_custom_call" | custom-call | tf_op jit(solution)/shard_map/transport/pallas_call | solution.py:361
  18.1 0.7 %copy.8 = f32[1,10,16,384]{3,2,1,0:T(8,128)} copy(f32[1,10,16,384]{3,2,1,0:T(8,128)S(1)} %bitcast.7) | data formatting | bytes 491520
where the time goes:
time: 19 us; the launch traced here: 18.8 us
  Pallas kernels  18.1 us (95%)
  local copies, waits for them, and re-layouts  0.7 us (4%)
    pallas_call x1, Pallas kernels, on_device(): pl.pallas_call(functools.partial(kernel, sizes), out_shape=pltpu.VMEM((ro...  18.1 us
    unnamed x1, local copies, waits for them, and re-layouts  0.7 us

commit v1 on v0

v1 whole, which is shorter than its diff:
```python
import functools

import jax
import jax.numpy as jnp
from jax import lax
from jax.experimental import pallas as pl
from jax.experimental.pallas import tpu as pltpu
from jax.sharding import PartitionSpec as P

BAND = 256
LANES = 128
SUB = 8
NODES = (-1.0, -0.4472135954999579, 0.4472135954999579, 1.0)
UNROLL = 4
MESH = pl.DeviceIdType.MESH


def basis(coord):
    terms = []
    for first in range(4):
        term = None
        scale = 1.0
        for other in range(4):
            if other != first:
                factor = coord - NODES[other]
                term = factor if term is None else term * factor
                scale = scale / (NODES[first] - NODES[other])
        terms.append(term * scale)
    return terms


def lookup(values, index):
    return jnp.take_along_axis(values, index, axis=1, mode="promise_in_bounds")


def wide(row):
    return jnp.broadcast_to(row, (SUB, LANES))


def kernel(
    sizes, tr, air_old, air_new, coord, slot, fetch, out,
    natural, stage, table, halo, side, along_a, along_b, mixed_a, mixed_b, places, masses, masses_old, coords, wanted,
    kept, message, heard, load_sem, halo_send, halo_recv, sum_send, sum_recv, ready,
):
    n_sfc, n_lev = sizes
    n_all = n_sfc * n_lev
    points = slot.shape[0]
    tracers, _, e_dev = tr.shape
    groups = e_dev // LANES
    row_groups = tracers * points // SUB
    halves = points // SUB
    flat = tracers * SUB
    mains = points
    rests = row_groups - mains
    band_groups = BAND // LANES
    me_s, me_l = lax.axis_index("sfc"), lax.axis_index("lev")
    me = me_s * n_lev + me_l

    barrier = pltpu.get_barrier_semaphore()
    right = (lax.rem(me_s + 1, n_sfc), me_l)
    left = (lax.rem(me_s + n_sfc - 1, n_sfc), me_l)

    def greet(sem, distance):
        for step in (distance, n_sfc - distance):
            pl.semaphore_signal(
                sem, inc=1, device_id=(lax.rem(me_s + step, n_sfc), me_l), device_id_type=MESH
            )

    def greet_levels(sem):
        for distance in range(1, n_lev):
            pl.semaphore_signal(
                sem, inc=1, device_id=(me_s, lax.rem(me_l + distance, n_lev)), device_id_type=MESH
            )

    greet(barrier, 1)
    greet_levels(barrier)

    def cols(group):
        return pl.ds(group * LANES, LANES)

    loads = []

    def load(source, target):
        copy = pltpu.make_async_copy(source, target, load_sem.at[len(loads)])
        copy.start()
        loads.append(copy)

    for g in range(groups):
        for h in range(halves):
            load(tr.at[:, pl.ds(h * SUB, SUB), cols(g)], natural.at[g, h])
        load(slot.at[:, cols(g)], places.at[g])
        load(coord.at[:, :, cols(g)], coords.at[g])
    for g in range(groups):
        load(air_old.at[:, cols(g)], masses_old.at[g])
        load(air_new.at[:, cols(g)], masses.at[g])
    load(fetch, wanted)

    def picked_rows(group):
        if group < mains:
            return pl.ds(group % SUB, SUB, stride=SUB)
        return pl.ds(SUB * SUB + (group - mains) % 2, SUB, stride=2)

    def half_of(h):
        return list(range(SUB * h, SUB * h + SUB)) + [mains + 2 * h, mains + 2 * h + 1]

    tall = tracers * points

    def split(pair):
        value = jnp.concatenate(pair, axis=0)
        high = value.astype(jnp.bfloat16)
        return high, (value - high.astype(jnp.float32)).astype(jnp.bfloat16)

    def prepare():
        for h in range(halves):
            for g in range(groups):
                block = natural.at[g, h].reshape(flat, LANES)
                rows = half_of(h)
                for r, other in zip(rows[::2], rows[1::2]):
                    pair = [block[picked_rows(r), :], block[picked_rows(other), :]]
                    high, low = split(pair)
                    alone = g % 2 == 0 and g + 1 == groups
                    for part, item in enumerate((high, low)):
                        start = (g // 2 * 2 + (0 if alone else part)) * tall + r * SUB
                        at = pl.ds(start, 2 * SUB)
                        table[at, cols(part if alone else g % 2)] = item
        for g in range(groups):
            for i, term in enumerate(basis(coords[g, 0])):
                along_a[i, g] = term
                for s in (0, 1, 4, 5):
                    mixed_a[i // 2, g, pl.ds(s + 2 * (i % 2), points, stride=SUB), :] = term
            for m, term in enumerate(basis(coords[g, 1])):
                along_b[m, g] = term
                for s in (0, 2, 4, 6):
                    mixed_b[m % 2, g, pl.ds(s + m // 2, points, stride=SUB), :] = term

    def shares(point, n, e):
        terms_b = [wide(along_b[m, e, pl.ds(n, 1), :]) for m in range(4)]
        interp = low = high = rest = low_rest = high_rest = None
        for i in range(4):
            inner = None
            for m in range(4):
                value = point(4 * i + m)
                low = value if low is None else jnp.minimum(low, value)
                high = value if high is None else jnp.maximum(high, value)
                scaled = terms_b[m] * value
                inner = scaled if inner is None else inner + scaled
            inner = inner * wide(along_a[i, e, pl.ds(n, 1), :])
            interp = inner if interp is None else interp + inner
        for h in range(halves):
            inner = None
            for q in range(2):
                value = point(mains + 2 * h + q)
                low_rest = value if low_rest is None else jnp.minimum(low_rest, value)
                high_rest = value if high_rest is None else jnp.maximum(high_rest, value)
                scaled = mixed_b[q, e, pl.ds(n * SUB, SUB), :] * value
                inner = scaled if inner is None else inner + scaled
            inner = inner * mixed_a[h, e, pl.ds(n * SUB, SUB), :]
            rest = inner if rest is None else rest + inner
        for shift in (1, 2):
            rest = rest + pltpu.roll(rest, SUB - shift, 0)
            low_rest = jnp.minimum(low_rest, pltpu.roll(low_rest, SUB - shift, 0))
            high_rest = jnp.maximum(high_rest, pltpu.roll(high_rest, SUB - shift, 0))
        return (interp, low, high), (rest, low_rest, high_rest)

    number = lax.broadcasted_iota(jnp.int32, (LANES, LANES), 0).astype(jnp.float32).astype(jnp.bfloat16)

    def chosen(n, e, number, group):
        columns = []
        for p in range(2):
            row = wide(places[e, pl.ds(n + p, 1), :])
            spot = jnp.where(row >> 7 == group, row & (LANES - 1), -1).astype(jnp.float32)
            spot = jnp.concatenate([spot, spot], axis=0).astype(jnp.bfloat16)
            match = number == jnp.concatenate([spot] * SUB, axis=0)
            columns.append(jnp.where(match, jnp.bfloat16(1), jnp.bfloat16(0)))
        return jnp.concatenate(columns, axis=1)

    def times(values, pick):
        return jnp.dot(values, pick, preferred_element_type=jnp.float32)

    def own_found(n, e, number):
        total = None
        for g in range(0, groups, 2):
            one = chosen(n, e, number, g)
            if g + 1 < groups:
                pick = jnp.concatenate([one, chosen(n, e, number, g + 1)], axis=0)
                both = times(table[pl.ds(g * tall, 2 * tall), :], pick)
                found = both[:tall] + both[tall:]
            else:
                pick = jnp.concatenate([one, one], axis=0)
                found = times(table[pl.ds(g * tall, tall), :], pick)
            total = found if total is None else total + found
        return total

    def side_found(at, k, n, e, number):
        one = chosen(n, e, number, groups + k)
        return times(side[at], jnp.concatenate([one, one], axis=0))

    def gather_pass(finder, first, i, carry):
        sums = list(carry)
        n = 2 * i
        for e in range(groups):
            found = finder(n, e, number)
            for p in range(2):
                def point(r):
                    return found[r * SUB : (r + 1) * SUB, p * LANES : (p + 1) * LANES]

                mass = wide(masses[e, pl.ds(n + p, 1), :])
                for b, (value, least, most) in enumerate(shares(point, n + p, e)):
                    clipped = jnp.minimum(jnp.maximum(value, least), most)
                    for q, kind in enumerate((clipped, most - clipped, clipped - least)):
                        sums[3 * b + q] = sums[3 * b + q] + mass * kind
                        if not first:
                            kind = kind + kept[b, q, n + p, :, cols(e)]
                        kept[b, q, n + p, :, cols(e)] = kind
        return tuple(sums)

    def receive(k, h, at):
        for g in range(band_groups):
            pltpu.make_async_copy(halo.at[k, g, h], halo.at[k, g, h], halo_recv.at[k, g, h]).wait()
        index = wide(wanted[pl.ds(k, 1), :]) - jnp.where(k == 0, e_dev - BAND, 0)
        index_low, index_high = index & (LANES - 1), index >> 7
        blocks = [halo.at[k, g, h].reshape(flat, LANES) for g in range(band_groups)]
        rows = half_of(h)
        for first, second in zip(rows[::2], rows[1::2]):
            pair = []
            for r in (first, second):
                value = lookup(blocks[0][picked_rows(r), :], index_low)
                for g in range(1, band_groups):
                    value = jnp.where(
                        index_high == g, lookup(blocks[g][picked_rows(r), :], index_low), value
                    )
                pair.append(value)
            for part, item in enumerate(split(pair)):
                side[at, pl.ds(first * SUB, 2 * SUB), cols(part)] = item

    for copy in loads:
        copy.wait()
    pl.semaphore_wait(barrier, n_lev + 1)
    sends = []
    for k, (target, start) in enumerate(((right, e_dev - BAND), (left, 0))):
        for h in range(halves):
            for g in range(band_groups):
                send = pltpu.make_async_remote_copy(
                    src_ref=natural.at[start // LANES + g, h],
                    dst_ref=halo.at[k, g, h],
                    send_sem=halo_send.at[k, g, h],
                    recv_sem=halo_recv.at[k, g, h],
                    device_id=target,
                    device_id_type=MESH,
                )
                send.start()
                sends.append(send)
    spans = [d for d in (1 << p for p in range(n_sfc)) if 2 * d < n_sfc]

    def next_round(r):
        if 0 < r <= len(spans):
            pl.semaphore_wait(ready.at[r - 1], 2)
        if r < len(spans):
            greet(ready.at[r], spans[r])
        elif r == len(spans):
            greet_levels(ready.at[r])
        else:
            pl.semaphore_wait(ready.at[r - 1], n_lev - 1)

    next_round(0)

    @pl.when(me_s == 0)
    def _():
        next_round(1)

    prepare()
    zero = jnp.zeros((SUB, LANES), jnp.float32)
    sums = lax.fori_loop(
        0, points // 2, functools.partial(gather_pass, own_found, True), (zero,) * 6, unroll=UNROLL
    )

    @pl.when(me_s != 0)
    def _():
        next_round(1)

    lane = lax.broadcasted_iota(jnp.int32, (SUB, LANES), 1)
    row = lax.broadcasted_iota(jnp.int32, (SUB, LANES), 0)
    old_main = jnp.zeros((SUB, LANES), jnp.float32)
    for j in range(mains):
        for g in range(groups):
            block = natural.at[g, j // SUB].reshape(flat, LANES)
            old_main += block[picked_rows(j), :] * wide(masses_old[g, pl.ds(j, 1), :])
    packed = jnp.where(lane == row, jnp.sum(old_main, axis=1, keepdims=True), 0.0)
    for t in range(SUB, tracers):
        product = sum(
            natural[g, h, t] * masses_old[g, pl.ds(h * SUB, SUB), :]
            for g in range(groups)
            for h in range(halves)
        )
        total = jnp.sum(jnp.sum(product, axis=1, keepdims=True), axis=0, keepdims=True)
        at = 4 * (t - SUB)
        packed = jnp.where((lane == 4 * SUB + row) & (row == at), total, packed)

    far = lax.rem(me_s, 2)
    for at, k in enumerate((1 - far, far)):
        for h in range(halves):
            receive(k, h, at)
        sums = lax.fori_loop(
            0,
            points // 2,
            functools.partial(gather_pass, functools.partial(side_found, at, k), False),
            sums,
            unroll=UNROLL,
        )
        if at == 0:
            for r in range(2, len(spans) + 1):
                next_round(r)

    for b in range(2):
        for q in range(3):
            total = jnp.sum(sums[3 * b + q], axis=1, keepdims=True)
            packed = jnp.where(lane == (4 * b + q + 1) * SUB + row, total, packed)
    packed = jnp.sum(packed, axis=0, keepdims=True)
    message[...] = packed

    next_round(len(spans) + 1)

    def tell(place, carry):
        other = place + jnp.where(place >= me, 1, 0)
        pltpu.make_async_remote_copy(
            src_ref=message,
            dst_ref=heard.at[me - jnp.where(place < me, 1, 0)],
            send_sem=sum_send,
            recv_sem=sum_recv,
            device_id=(lax.div(other, n_lev), lax.rem(other, n_lev)),
            device_id_type=MESH,
        ).start()
        return carry

    lax.fori_loop(0, n_all - 1, tell, 0)
    pltpu.make_async_copy(heard, heard, sum_recv).wait()
    total = packed
    for k in range(n_all - 1) if n_all <= 64 else ():
        total = total + heard[k]
    if n_all > 64:
        total = lax.fori_loop(0, n_all - 1, lambda k, acc: acc + heard[k], total)

    old, clip, up, down = [
        wide(total) if q == 0 else pltpu.roll(wide(total), LANES - q * SUB, 1) for q in range(4)
    ]
    shortfall = old - clip
    raised = jnp.where(shortfall >= 0, shortfall / up, 0.0)
    lowered = jnp.where(shortfall >= 0, 0.0, shortfall / down)
    gains = []
    for b in range(2):
        pair = []
        for gain in (raised, lowered):
            column = jnp.where(lane == 4 * b * SUB + row, gain, 0.0)
            pair.append(jnp.broadcast_to(jnp.sum(column, axis=1, keepdims=True), (SUB, LANES)))
        gains.append(pair)

    def fix(n, carry):
        for e in range(groups):
            done = []
            for b in range(2):
                clipped, up, down = [kept[b, q, n, :, cols(e)] for q in range(3)]
                done.append(clipped + (gains[b][0] * up + gains[b][1] * down))
            stage[e, pl.ds(n, SUB, stride=points), :] = done[0]
            for t in range(SUB, tracers):
                at = 4 * (t - SUB)
                stage[e, pl.ds(t * points + n, 1), :] = done[1][at : at + 1]
        return carry

    lax.fori_loop(0, points, fix, 0, unroll=2)
    for g in range(groups):
        out[:, cols(g)] = stage[g]
    for send in sends:
        send.wait_send()
    pltpu.make_async_copy(heard, heard, sum_send).wait()


def solution(mesh):
    sizes = (mesh.shape["sfc"], mesh.shape["lev"])
    n_all = sizes[0] * sizes[1]

    def on_device(tracer_old, air_old, air_new, dep_coord, dep_slot, fetch_list):
        levels, tracers, points, e_dev = tracer_old.shape
        cap = fetch_list.shape[2]
        assert levels == 1 and cap == LANES and tracers == SUB + 2 and points == 16
        rows = tracers * points
        groups, halves = e_dev // LANES, points // SUB
        vmem = pl.BlockSpec(memory_space=pltpu.VMEM)
        result = pl.pallas_call(
            functools.partial(kernel, sizes),
            out_shape=pltpu.VMEM((rows, e_dev), jnp.float32),
            in_specs=[pl.BlockSpec(memory_space=pl.ANY)] * 6,
            out_specs=vmem,
            scratch_shapes=[
                pltpu.VMEM((groups, halves, tracers, SUB, LANES), jnp.float32),
                pltpu.VMEM((groups, rows, LANES), jnp.float32),
                pltpu.VMEM((groups * rows, 2 * LANES), jnp.bfloat16),
                pltpu.VMEM((2, BAND // LANES, halves, tracers, SUB, LANES), jnp.float32),
                pltpu.VMEM((2, rows, 2 * LANES), jnp.bfloat16),
                pltpu.VMEM((4, groups, points, LANES), jnp.float32),
                pltpu.VMEM((4, groups, points, LANES), jnp.float32),
                pltpu.VMEM((2, groups, points * SUB, LANES), jnp.float32),
                pltpu.VMEM((2, groups, points * SUB, LANES), jnp.float32),
                pltpu.VMEM((groups, points, LANES), jnp.int32),
                pltpu.VMEM((groups, points, LANES), jnp.float32),
                pltpu.VMEM((groups, points, LANES), jnp.float32),
                pltpu.VMEM((groups, 2, points, LANES), jnp.float32),
                pltpu.VMEM((2, cap), jnp.int32),
                pltpu.VMEM((2, 3, points, SUB, e_dev), jnp.float32),
                pltpu.VMEM((1, LANES), jnp.float32),
                pltpu.VMEM((n_all - 1, 1, LANES), jnp.float32),
                pltpu.SemaphoreType.DMA(((4 + halves) * groups + 1,)),
                pltpu.SemaphoreType.DMA((2, BAND // LANES, halves)),
                pltpu.SemaphoreType.DMA((2, BAND // LANES, halves)),
                pltpu.SemaphoreType.DMA,
                pltpu.SemaphoreType.DMA,
                pltpu.SemaphoreType.REGULAR((sizes[0].bit_length(),)),
            ],
            compiler_params=pltpu.CompilerParams(collective_id=0, has_side_effects=True),
            name="transport",
        )(
            tracer_old.reshape(tracers, points, e_dev),
            air_old.reshape(points, e_dev),
            air_new.reshape(points, e_dev),
            dep_coord.reshape(2, points, e_dev),
            dep_slot.reshape(points, e_dev),
            fetch_list.reshape(2, cap),
        )
        return result.reshape(levels, tracers, points, e_dev)

    return jax.shard_map(
        on_device,
        mesh=mesh,
        in_specs=(
            P("lev", None, None, "sfc"),
            P("lev", None, "sfc"),
            P("lev", None, "sfc"),
            P(None, "lev", None, "sfc"),
            P("lev", None, "sfc"),
            P("sfc", None, None),
        ),
        out_specs=P("lev", None, None, "sfc"),
        check_vma=False,
    )
```

time: 19 us -> 17.3 us (0.911)
  Pallas kernels: 18.1 us -> 16.4 us
    pallas_call x1, Pallas kernels: 18.1 us -> 16.4 us  [on_device(): pl.pallas_call(functools.partial(kernel, sizes), out_shape=pltpu.VMEM((ro...]
where the time goes in v1:
time: 17.3 us; the launch traced here: 17.1 us
  Pallas kernels  16.4 us (95%)
  local copies, waits for them, and re-layouts  0.7 us (4%)
    pallas_call x1, Pallas kernels, on_device(): pl.pallas_call(functools.partial(kernel, sizes), out_shape=pltpu.VMEM((ro...  16.4 us
    unnamed x1, local copies, waits for them, and re-layouts  0.7 us

profile of v1, /device:TPU:0, one launch (start us, length us, event | category | flops | bytes accessed | tf_op | source)
XLA Modules:
  0.0 17.1 jit_solution(7670600102720648350)
XLA Ops:
  0.0 16.4 %transport.1 = f32[160,384]{1,0:T(8,128)S(1)} custom-call(f32[10,16,384]{2,1,0:T(8,128)} %bitcast.8, f32[16,384]{1,0:T(8,128)} %bitcast.10, f32[16,384]{1,0:T(8,128)} %bitcast.11, f32[2,16,384]{2,1,0:T(8,128)} %bitcast.9, s32[16,384]{1,0:T(8,128)} %bitcast.12, s32[2,128]{1,0:T(2,128)} %bitcast.13), custom_call_target="tpu_custom_call" | custom-call | tf_op jit(solution)/shard_map/transport/pallas_call | solution.py:388
  16.4 0.7 %copy.8 = f32[1,10,16,384]{3,2,1,0:T(8,128)} copy(f32[1,10,16,384]{3,2,1,0:T(8,128)S(1)} %bitcast.7) | data formatting | bytes 491520

commit v2 on v1

v2 whole, which is shorter than its diff:
```python
import functools
import math

import jax
import jax.numpy as jnp
from jax import lax
from jax.experimental import pallas as pl
from jax.experimental.pallas import tpu as pltpu
from jax.sharding import PartitionSpec as P

BAND = 256
LANES = 128
SUB = 8
NODES = (-1.0, -0.4472135954999579, 0.4472135954999579, 1.0)
UNROLL = 8
MESH = pl.DeviceIdType.MESH


def basis(coord):
    terms = []
    for first in range(4):
        term = None
        scale = 1.0
        for other in range(4):
            if other != first:
                factor = coord - NODES[other]
                term = factor if term is None else term * factor
                scale = scale / (NODES[first] - NODES[other])
        terms.append(term * scale)
    return terms


def cubic(values):
    outer, inner = values[3] + values[0], values[2] + values[1]
    wide_odd, near_odd = values[3] - values[0], (values[2] - values[1]) * math.sqrt(5.0)
    return [
        0.625 * inner - 0.125 * outer,
        0.625 * near_odd - 0.125 * wide_odd,
        0.625 * (outer - inner),
        0.625 * (wide_odd - near_odd),
    ]


def horner(terms, at):
    total = terms[3]
    for term in terms[2::-1]:
        total = total * at + term
    return total


def lookup(values, index):
    return jnp.take_along_axis(values, index, axis=1, mode="promise_in_bounds")


def wide(row):
    return jnp.broadcast_to(row, (SUB, LANES))


def split(pair):
    value = jnp.concatenate(pair, axis=0)
    high = value.astype(jnp.bfloat16)
    return high, (value - high.astype(jnp.float32)).astype(jnp.bfloat16)


def folded(values, combine):
    for shift in (1, 2):
        values = combine(values, pltpu.roll(values, SUB - shift, 0))
    return values


def kernel(
    sizes, tr, air_old, air_new, coord, slot, fetch, out,
    natural, stage, table, spare, halo, side, plain, picks, along, places, masses, masses_old, coords, wanted,
    kept, gains, message, heard, load_sem, halo_send, halo_recv, sum_send, sum_recv, ready,
):
    n_sfc, n_lev = sizes
    n_all = n_sfc * n_lev
    points = slot.shape[0]
    tracers, _, e_dev = tr.shape
    groups = e_dev // LANES
    halves = points // SUB
    mains = points
    line = 4
    flat = tracers * points
    kinds = mains + line + 4
    tall = kinds * SUB
    band_groups = BAND // LANES
    steps = points // 2
    me_s, me_l = lax.axis_index("sfc"), lax.axis_index("lev")
    me = me_s * n_lev + me_l
    right = (lax.rem(me_s + 1, n_sfc), me_l)
    left = (lax.rem(me_s + n_sfc - 1, n_sfc), me_l)
    hub_s, hub_l = n_sfc - 1, n_lev - 1
    at_hub = me == n_all - 1
    barrier = pltpu.get_barrier_semaphore()

    def signal(sem, s, l):
        pl.semaphore_signal(sem, inc=1, device_id=(s, l), device_id_type=MESH)

    for other_s, other_l in (right, left):

        @pl.when(jnp.logical_or(other_s != hub_s, other_l != hub_l))
        def _():
            signal(barrier, other_s, other_l)

    @pl.when(jnp.logical_not(at_hub))
    def _():
        signal(barrier, hub_s, hub_l)

    def cols(group):
        return pl.ds(group * LANES, LANES)

    loads = []

    def load(source, target):
        copy = pltpu.make_async_copy(source, target, load_sem.at[len(loads)])
        copy.start()
        loads.append(copy)

    for g in range(groups):
        load(tr.at[:, :, cols(g)], natural.at[g])
    for g in range(groups):
        load(slot.at[:, cols(g)], places.at[g])
        load(coord.at[:, :, cols(g)], coords.at[g])
    for g in range(groups):
        load(air_old.at[:, cols(g)], masses_old.at[g])
        load(air_new.at[:, cols(g)], masses.at[g])
    load(fetch, wanted)

    def picked_rows(r):
        if r < mains:
            return pl.ds(r, SUB, stride=points)
        return pl.ds(SUB * points + (r - mains), SUB, stride=line)

    def as_rows(main, rest):
        ranges = []
        for combine in (jnp.minimum, jnp.maximum):
            ranges.append(functools.reduce(combine, main))
        for combine in (jnp.minimum, jnp.maximum):
            ranges.append(folded(functools.reduce(combine, rest), combine))
        along_b = [cubic(main[line * i : line * i + line]) for i in range(line)]
        along_a = [cubic([along_b[i][m] for i in range(line)]) for m in range(line)]
        return [along_a[m][i] for i in range(line) for m in range(line)] + cubic(rest) + ranges

    def prepare():
        for g in range(groups):
            block = natural.at[g].reshape(flat, LANES)
            found = [block[picked_rows(r), :] for r in range(mains + line)]
            rows = as_rows(found[:mains], found[mains:])
            if g == groups - 1:
                for r, item in enumerate(rows):
                    spare[pl.ds(r * SUB, SUB), :] = item
                continue
            for r in range(0, kinds, 2):
                for part, item in enumerate(split(rows[r : r + 2])):
                    at = pl.ds((g // 2 * 2 + part) * tall + r * SUB, 2 * SUB)
                    table[at, cols(g % 2)] = item
        for g in range(groups):
            for i, term in enumerate(basis(coords[g, 0])):
                for s in (i, i + line):
                    along[g, pl.ds(s, points, stride=SUB), :] = term

    def interpolate(point, n, e):
        at_a, at_b = [wide(coords[e, x, pl.ds(n, 1), :]) for x in range(2)]
        inner = [horner([point(line * i + m) for m in range(line)], at_b) for i in range(line)]
        interp = horner(inner, at_a)
        rest = horner([point(mains + m) for m in range(line)], at_b)
        rest = folded(rest * along[e, pl.ds(n * SUB, SUB), :], jnp.add)
        low, high, low_rest, high_rest = [point(mains + line + x) for x in range(4)]
        return (interp, low, high), (rest, low_rest, high_rest)

    number = lax.broadcasted_iota(jnp.int32, (LANES, LANES), 0).astype(jnp.float32).astype(jnp.bfloat16)

    def chosen(n, e, group):
        columns = []
        for p in range(2):
            row = wide(places[e, pl.ds(n + p, 1), :])
            spot = jnp.where(row >> 7 == group, row & (LANES - 1), -1).astype(jnp.float32)
            spot = jnp.concatenate([spot, spot], axis=0).astype(jnp.bfloat16)
            match = number == jnp.concatenate([spot] * SUB, axis=0)
            columns.append(jnp.where(match, jnp.bfloat16(1), jnp.bfloat16(0)))
        return jnp.concatenate(columns, axis=1)

    def times(values, pick):
        return jnp.dot(values, pick, preferred_element_type=jnp.float32)

    def own_found(n, e):
        total = None
        for g in range(0, groups - 1, 2):
            pick = jnp.concatenate([chosen(n, e, g + x) for x in range(2)], axis=0)
            both = times(table[pl.ds(g * tall, 2 * tall), :], pick)
            found = both[:tall] + both[tall:]
            total = found if total is None else total + found
        return total

    def near_found(k, n, e):
        one = chosen(n, e, groups + k)
        return times(side[0], jnp.concatenate([one, one], axis=0))

    def far_found(n, e):
        one = picks[n // 2, e]
        return times(side[1], jnp.concatenate([one, one], axis=0))

    def foresee(k, i, carry):
        for e in range(groups - 1):
            picks[i, e] = chosen(2 * i, e, groups + k)
        return carry

    def gather_pass(finder, values, group, turn, i, carry):
        sums = list(carry)
        n = 2 * i
        for e in range(groups):
            by_lookup = turn > 0 and e == groups - 1
            found = None if by_lookup else finder(n, e)
            for p in range(2):
                index = wide(places[e, pl.ds(n + p, 1), :])
                low_index, mine = index & (LANES - 1), (index >> 7) == group

                def point(r):
                    here = pl.ds(r * SUB, SUB)
                    if found is not None:
                        value = found[r * SUB : (r + 1) * SUB, p * LANES : (p + 1) * LANES]
                        if turn > 0:
                            return value
                        return jnp.where(mine, lookup(values[here, :], low_index), value)
                    return lookup(values[here, :], low_index)

                mass = wide(masses[e, pl.ds(n + p, 1), :])
                for b, (value, least, most) in enumerate(interpolate(point, n + p, e)):
                    clipped = jnp.minimum(jnp.maximum(value, least), most)
                    for q, kind in enumerate((clipped, most - clipped, clipped - least)):
                        if by_lookup:
                            kind = jnp.where(mine, kind, 0.0)
                        sums[3 * b + q] = sums[3 * b + q] + mass * kind
                        kept[turn, b, q, n + p, :, cols(e)] = kind
        return tuple(sums)

    def receive(k, at):
        index = wide(wanted[pl.ds(k, 1), :]) - jnp.where(k == 0, e_dev - BAND, 0)
        index_low, index_high = index & (LANES - 1), index >> 7
        blocks = [halo.at[k, g].reshape(flat, LANES) for g in range(band_groups)]
        found = []

        def select(r):
            value = lookup(blocks[0][picked_rows(r), :], index_low)
            for g in range(1, band_groups):
                value = jnp.where(
                    index_high == g, lookup(blocks[g][picked_rows(r), :], index_low), value
                )
            found.append(value)

        for h in range(halves):
            for g in range(band_groups):
                landed = halo.at[k, g, :, pl.ds(h * SUB, SUB), :]
                pltpu.make_async_copy(landed, landed, halo_recv.at[k, g, h]).wait()
            for r in range(h * SUB, h * SUB + SUB):
                select(r)
        for r in range(mains, mains + line):
            select(r)
        rows = as_rows(found[:mains], found[mains:])
        for r in range(0, kinds, 2):
            for part, item in enumerate(split(rows[r : r + 2])):
                side[at, pl.ds(r * SUB, 2 * SUB), cols(part)] = item
        for r, item in enumerate(rows):
            plain[at, pl.ds(r * SUB, SUB), :] = item

    for copy in loads:
        copy.wait()
    pl.semaphore_wait(barrier, jnp.where(at_hub, n_all - 1, 2))
    sends = []
    for k, (target, start) in enumerate(((right, e_dev - BAND), (left, 0))):
        for h in range(halves):
            for g in range(band_groups):
                part = pl.ds(h * SUB, SUB)
                send = pltpu.make_async_remote_copy(
                    src_ref=natural.at[start // LANES + g, :, part, :],
                    dst_ref=halo.at[k, g, :, part, :],
                    send_sem=halo_send.at[k, g, h],
                    recv_sem=halo_recv.at[k, g, h],
                    device_id=target,
                    device_id_type=MESH,
                )
                send.start()
                sends.append(send)

    @pl.when(at_hub)
    def _():
        def admit(other, carry):
            signal(ready, lax.div(other, n_lev), lax.rem(other, n_lev))
            return carry

        lax.fori_loop(0, n_all - 1, admit, 0)

    prepare()
    zero = jnp.zeros((SUB, LANES), jnp.float32)
    sums = lax.fori_loop(
        0, steps, functools.partial(gather_pass, own_found, spare, groups - 1, 0), (zero,) * 6, unroll=UNROLL
    )

    lane = lax.broadcasted_iota(jnp.int32, (SUB, LANES), 1)
    row = lax.broadcasted_iota(jnp.int32, (SUB, LANES), 0)
    old_main = jnp.zeros((SUB, LANES), jnp.float32)
    for g in range(groups):
        block = natural.at[g].reshape(flat, LANES)
        for j in range(mains):
            old_main += block[picked_rows(j), :] * wide(masses_old[g, pl.ds(j, 1), :])
    packed = jnp.where(lane == row, jnp.sum(old_main, axis=1, keepdims=True), 0.0)
    for t in range(SUB, tracers):
        product = sum(natural[g, t] * masses_old[g] for g in range(groups))
        total = jnp.sum(jnp.sum(product, axis=1, keepdims=True), axis=0, keepdims=True)
        at = line * (t - SUB)
        packed = jnp.where((lane == 4 * SUB + row) & (row == at), total, packed)

    far = lax.rem(me_s, 2)
    near = 1 - far
    receive(near, 0)
    sums = lax.fori_loop(
        0,
        steps,
        functools.partial(gather_pass, functools.partial(near_found, near), plain.at[0], groups + near, 1),
        sums,
        unroll=UNROLL,
    )
    lax.fori_loop(0, steps, functools.partial(foresee, far), 0, unroll=2)
    receive(far, 1)
    sums = lax.fori_loop(
        0,
        steps,
        functools.partial(gather_pass, far_found, plain.at[1], groups + far, 2),
        sums,
        unroll=UNROLL,
    )

    for b in range(2):
        for q in range(3):
            total = jnp.sum(sums[3 * b + q], axis=1, keepdims=True)
            packed = jnp.where(lane == (4 * b + q + 1) * SUB + row, total, packed)
    packed = jnp.sum(packed, axis=0, keepdims=True)
    message[...] = packed

    @pl.when(jnp.logical_not(at_hub))
    def _():
        pl.semaphore_wait(ready, 1)

    def tell(place, carry):
        other = place + jnp.where(place >= me, 1, 0)
        pltpu.make_async_remote_copy(
            src_ref=message,
            dst_ref=heard.at[me - jnp.where(place < me, 1, 0)],
            send_sem=sum_send,
            recv_sem=sum_recv,
            device_id=(lax.div(other, n_lev), lax.rem(other, n_lev)),
            device_id_type=MESH,
        ).start()
        return carry

    lax.fori_loop(0, n_all - 1, tell, 0)

    def arrange(n, carry):
        for e in range(groups):
            for q in range(3):
                main, rest = [
                    sum(kept[turn, b, q, n, :, cols(e)] for turn in range(3)) for b in range(2)
                ]
                stage[q, e, pl.ds(n, SUB, stride=points), :] = main
                for t in range(SUB, tracers):
                    at = line * (t - SUB)
                    stage[q, e, pl.ds(t * points + n, 1), :] = rest[at : at + 1]
        return carry

    lax.fori_loop(0, points, arrange, 0, unroll=2)
    for send in sends:
        send.wait_send()
    pltpu.make_async_copy(heard, heard, sum_recv).wait()
    total = packed
    for k in range(n_all - 1) if n_all <= 64 else ():
        total = total + heard[k]
    if n_all > 64:
        total = lax.fori_loop(0, n_all - 1, lambda k, acc: acc + heard[k], total)

    old, clip, up, down = [
        wide(total) if q == 0 else pltpu.roll(wide(total), LANES - q * SUB, 1) for q in range(4)
    ]
    shortfall = old - clip
    raised = jnp.where(shortfall >= 0, shortfall / up, 0.0)
    lowered = jnp.where(shortfall >= 0, 0.0, shortfall / down)
    for b in range(2):
        for x, gain in enumerate((raised, lowered)):
            column = jnp.where(lane == 4 * b * SUB + row, gain, 0.0)
            gains[b, x] = jnp.broadcast_to(jnp.sum(column, axis=1, keepdims=True), (SUB, LANES))
    for t in range(tracers):
        b, at = (0, t) if t < SUB else (1, line * (t - SUB))
        up, down = [wide(gains[b, x, pl.ds(at, 1), :]) for x in range(2)]
        for g in range(groups):
            for h in range(halves):
                rows = pl.ds(t * points + h * SUB, SUB)
                moved = up * stage[1, g, rows, :] + down * stage[2, g, rows, :]
                out[rows, cols(g)] = stage[0, g, rows, :] + moved
    pltpu.make_async_copy(heard, heard, sum_send).wait()


def solution(mesh):
    sizes = (mesh.shape["sfc"], mesh.shape["lev"])
    n_all = sizes[0] * sizes[1]

    def on_device(tracer_old, air_old, air_new, dep_coord, dep_slot, fetch_list):
        levels, tracers, points, e_dev = tracer_old.shape
        cap = fetch_list.shape[2]
        assert levels == 1 and cap == LANES and tracers == SUB + 2 and points == 16
        assert e_dev // LANES % 2 == 1
        rows = tracers * points
        groups, halves = e_dev // LANES, points // SUB
        tall = (points + 8) * SUB
        vmem = pl.BlockSpec(memory_space=pltpu.VMEM)
        result = pl.pallas_call(
            functools.partial(kernel, sizes),
            out_shape=pltpu.VMEM((rows, e_dev), jnp.float32),
            in_specs=[pl.BlockSpec(memory_space=pl.ANY)] * 6,
            out_specs=vmem,
            scratch_shapes=[
                pltpu.VMEM((groups, tracers, points, LANES), jnp.float32),
                pltpu.VMEM((3, groups, rows, LANES), jnp.float32),
                pltpu.VMEM(((groups - 1) * tall, 2 * LANES), jnp.bfloat16),
                pltpu.VMEM((tall, LANES), jnp.float32),
                pltpu.VMEM((2, BAND // LANES, tracers, points, LANES), jnp.float32),
                pltpu.VMEM((2, tall, 2 * LANES), jnp.bfloat16),
                pltpu.VMEM((2, tall, LANES), jnp.float32),
                pltpu.VMEM((points // 2, groups - 1, LANES, 2 * LANES), jnp.bfloat16),
                pltpu.VMEM((groups, points * SUB, LANES), jnp.float32),
                pltpu.VMEM((groups, points, LANES), jnp.int32),
                pltpu.VMEM((groups, points, LANES), jnp.float32),
                pltpu.VMEM((groups, points, LANES), jnp.float32),
                pltpu.VMEM((groups, 2, points, LANES), jnp.float32),
                pltpu.VMEM((2, cap), jnp.int32),
                pltpu.VMEM((3, 2, 3, points, SUB, e_dev), jnp.float32),
                pltpu.VMEM((2, 2, SUB, LANES), jnp.float32),
                pltpu.VMEM((1, LANES), jnp.float32),
                pltpu.VMEM((n_all - 1, 1, LANES), jnp.float32),
                pltpu.SemaphoreType.DMA((5 * groups + 1,)),
                pltpu.SemaphoreType.DMA((2, BAND // LANES, halves)),
                pltpu.SemaphoreType.DMA((2, BAND // LANES, halves)),
                pltpu.SemaphoreType.DMA,
                pltpu.SemaphoreType.DMA,
                pltpu.SemaphoreType.REGULAR,
            ],
            compiler_params=pltpu.CompilerParams(collective_id=0, has_side_effects=True),
            name="transport",
        )(
            tracer_old.reshape(tracers, points, e_dev),
            air_old.reshape(points, e_dev),
            air_new.reshape(points, e_dev),
            dep_coord.reshape(2, points, e_dev),
            dep_slot.reshape(points, e_dev),
            fetch_list.reshape(2, cap),
        )
        return result.reshape(levels, tracers, points, e_dev)

    return jax.shard_map(
        on_device,
        mesh=mesh,
        in_specs=(
            P("lev", None, None, "sfc"),
            P("lev", None, "sfc"),
            P("lev", None, "sfc"),
            P(None, "lev", None, "sfc"),
            P("lev", None, "sfc"),
            P("sfc", None, None),
        ),
        out_specs=P("lev", None, None, "sfc"),
        check_vma=False,
    )
```

time: 17.3 us -> 16.5 us (0.954)
  Pallas kernels: 16.4 us -> 15.6 us
    pallas_call x1, Pallas kernels: 16.4 us -> 15.6 us  [on_device(): pl.pallas_call(functools.partial(kernel, sizes), out_shape=pltpu.VMEM((ro...]
where the time goes in v2:
time: 16.5 us; the launch traced here: 16.3 us
  Pallas kernels  15.6 us (95%)
  local copies, waits for them, and re-layouts  0.7 us (4%)
    pallas_call x1, Pallas kernels, on_device(): pl.pallas_call(functools.partial(kernel, sizes), out_shape=pltpu.VMEM((ro...  15.6 us
    unnamed x1, local copies, waits for them, and re-layouts  0.7 us

profile of v2, /device:TPU:0, one launch (start us, length us, event | category | flops | bytes accessed | tf_op | source)
XLA Modules:
  0.0 16.3 jit_solution(3641501181697063675)
XLA Ops:
  0.0 15.6 %transport.1 = f32[160,384]{1,0:T(8,128)S(1)} custom-call(f32[10,16,384]{2,1,0:T(8,128)} %bitcast.8, f32[16,384]{1,0:T(8,128)} %bitcast.10, f32[16,384]{1,0:T(8,128)} %bitcast.11, f32[2,16,384]{2,1,0:T(8,128)} %bitcast.9, s32[16,384]{1,0:T(8,128)} %bitcast.12, s32[2,128]{1,0:T(2,128)} %bitcast.13), custom_call_target="tpu_custom_call" | custom-call | tf_op jit(solution)/shard_map/transport/pallas_call | solution.py:415
  15.6 0.7 %copy.8 = f32[1,10,16,384]{3,2,1,0:T(8,128)} copy(f32[1,10,16,384]{3,2,1,0:T(8,128)S(1)} %bitcast.7) | data formatting | bytes 491520

commit v3 on v2

--- a/solution.py
+++ b/solution.py
@@ -70,7 +70,7 @@
 
 def kernel(
     sizes, tr, air_old, air_new, coord, slot, fetch, out,
-    natural, stage, table, spare, halo, side, plain, picks, along, places, masses, masses_old, coords, wanted,
+    fields, stage, table, spare, halo, side, plain, picks, along, places, wanted,
     kept, gains, message, heard, load_sem, halo_send, halo_recv, sum_send, sum_recv, ready,
 ):
     n_sfc, n_lev = sizes
@@ -84,6 +84,7 @@
     flat = tracers * points
     kinds = mains + line + 4
     tall = kinds * SUB
+    main_tall = (mains + 2) * SUB
     band_groups = BAND // LANES
     steps = points // 2
     me_s, me_l = lax.axis_index("sfc"), lax.axis_index("lev")
@@ -92,6 +93,8 @@
     left = (lax.rem(me_s + n_sfc - 1, n_sfc), me_l)
     hub_s, hub_l = n_sfc - 1, n_lev - 1
     at_hub = me == n_all - 1
+    far = lax.rem(me_s, 2)
+    near = 1 - far
     barrier = pltpu.get_barrier_semaphore()
 
     def signal(sem, s, l):
@@ -110,43 +113,41 @@
     def cols(group):
         return pl.ds(group * LANES, LANES)
 
-    loads = []
-
-    def load(source, target):
-        copy = pltpu.make_async_copy(source, target, load_sem.at[len(loads)])
-        copy.start()
-        loads.append(copy)
-
+    def load(source, target, sem):
+        pltpu.make_async_copy(source, target, load_sem.at[sem]).start()
+
+    at_coord, at_new, at_old = tracers, tracers + 2, tracers + 3
     for g in range(groups):
-        load(tr.at[:, :, cols(g)], natural.at[g])
+        load(tr.at[:, :, cols(g)], fields.at[g, pl.ds(0, tracers)], 0)
     for g in range(groups):
-        load(slot.at[:, cols(g)], places.at[g])
-        load(coord.at[:, :, cols(g)], coords.at[g])
+        load(slot.at[:, cols(g)], places.at[g], 1)
+        load(coord.at[:, :, cols(g)], fields.at[g, pl.ds(at_coord, 2)], 0)
     for g in range(groups):
-        load(air_old.at[:, cols(g)], masses_old.at[g])
-        load(air_new.at[:, cols(g)], masses.at[g])
-    load(fetch, wanted)
+        load(air_old.at[:, cols(g)], fields.at[g, at_old], 0)
+        load(air_new.at[:, cols(g)], fields.at[g, at_new], 0)
+    load(fetch, wanted, 2)
 
     def picked_rows(r):
         if r < mains:
             return pl.ds(r, SUB, stride=points)
         return pl.ds(SUB * points + (r - mains), SUB, stride=line)
 
-    def as_rows(main, rest):
-        ranges = []
-        for combine in (jnp.minimum, jnp.maximum):
-            ranges.append(functools.reduce(combine, main))
-        for combine in (jnp.minimum, jnp.maximum):
-            ranges.append(folded(functools.reduce(combine, rest), combine))
+    def main_rows(main):
         along_b = [cubic(main[line * i : line * i + line]) for i in range(line)]
         along_a = [cubic([along_b[i][m] for i in range(line)]) for m in range(line)]
-        return [along_a[m][i] for i in range(line) for m in range(line)] + cubic(rest) + ranges
+        ranges = [functools.reduce(combine, main) for combine in (jnp.minimum, jnp.maximum)]
+        return [along_a[m][i] for i in range(line) for m in range(line)] + ranges
+
+    def rest_rows(rest):
+        return cubic(rest) + [
+            folded(functools.reduce(combine, rest), combine) for combine in (jnp.minimum, jnp.maximum)
+        ]
 
     def prepare():
         for g in range(groups):
-            block = natural.at[g].reshape(flat, LANES)
+            block = fields.at[g].reshape((tracers + 4) * points, LANES)
             found = [block[picked_rows(r), :] for r in range(mains + line)]
-            rows = as_rows(found[:mains], found[mains:])
+            rows = main_rows(found[:mains]) + rest_rows(found[mains:])
             if g == groups - 1:
                 for r, item in enumerate(rows):
                     spare[pl.ds(r * SUB, SUB), :] = item
@@ -156,18 +157,18 @@
                     at = pl.ds((g // 2 * 2 + part) * tall + r * SUB, 2 * SUB)
                     table[at, cols(g % 2)] = item
         for g in range(groups):
-            for i, term in enumerate(basis(coords[g, 0])):
+            for i, term in enumerate(basis(fields[g, at_coord])):
                 for s in (i, i + line):
                     along[g, pl.ds(s, points, stride=SUB), :] = term
 
-    def interpolate(point, n, e):
-        at_a, at_b = [wide(coords[e, x, pl.ds(n, 1), :]) for x in range(2)]
-        inner = [horner([point(line * i + m) for m in range(line)], at_b) for i in range(line)]
-        interp = horner(inner, at_a)
-        rest = horner([point(mains + m) for m in range(line)], at_b)
+    def interpolate(point, n, e, b):
+        at_a, at_b = [wide(fields[e, at_coord + x, pl.ds(n, 1), :]) for x in range(2)]
+        if b == 0:
+            inner = [horner([point(line * i + m) for m in range(line)], at_b) for i in range(line)]
+            return horner(inner, at_a), point(mains), point(mains + 1)
+        rest = horner([point(mains + 2 + m) for m in range(line)], at_b)
         rest = folded(rest * along[e, pl.ds(n * SUB, SUB), :], jnp.add)
-        low, high, low_rest, high_rest = [point(mains + line + x) for x in range(4)]
-        return (interp, low, high), (rest, low_rest, high_rest)
+        return rest, point(mains + 2 + line), point(mains + 3 + line)
 
     number = lax.broadcasted_iota(jnp.int32, (LANES, LANES), 0).astype(jnp.float32).astype(jnp.bfloat16)
 
@@ -199,18 +200,18 @@
 
     def far_found(n, e):
         one = picks[n // 2, e]
-        return times(side[1], jnp.concatenate([one, one], axis=0))
+        return times(side[1, pl.ds(0, main_tall), :], jnp.concatenate([one, one], axis=0))
 
     def foresee(k, i, carry):
         for e in range(groups - 1):
             picks[i, e] = chosen(2 * i, e, groups + k)
         return carry
 
-    def gather_pass(finder, values, group, turn, i, carry):
+    def gather_pass(finder, values, group, turn, parts, i, carry):
         sums = list(carry)
         n = 2 * i
         for e in range(groups):
-            by_lookup = turn > 0 and e == groups - 1
+            by_lookup = finder is None or (turn > 0 and e == groups - 1)
             found = None if by_lookup else finder(n, e)
             for p in range(2):
                 index = wide(places[e, pl.ds(n + p, 1), :])
@@ -225,8 +226,9 @@
                         return jnp.where(mine, lookup(values[here, :], low_index), value)
                     return lookup(values[here, :], low_index)
 
-                mass = wide(masses[e, pl.ds(n + p, 1), :])
-                for b, (value, least, most) in enumerate(interpolate(point, n + p, e)):
+                mass = wide(fields[e, at_new, pl.ds(n + p, 1), :])
+                for b in parts:
+                    value, least, most = interpolate(point, n + p, e, b)
                     clipped = jnp.minimum(jnp.maximum(value, least), most)
                     for q, kind in enumerate((clipped, most - clipped, clipped - least)):
                         if by_lookup:
@@ -235,53 +237,64 @@
                         kept[turn, b, q, n + p, :, cols(e)] = kind
         return tuple(sums)
 
-    def receive(k, at):
+    def pieces():
+        yield pl.ds(SUB, tracers - SUB), pl.ds(0, points)
+        for h in range(halves):
+            yield pl.ds(0, SUB), pl.ds(h * SUB, SUB)
+
+    def arrived(k, piece):
+        landed = halo.at[(k, slice(None), *list(pieces())[piece])]
+        pltpu.make_async_copy(landed, landed, halo_recv.at[k, piece]).wait()
+
+    def select(k, rows):
         index = wide(wanted[pl.ds(k, 1), :]) - jnp.where(k == 0, e_dev - BAND, 0)
         index_low, index_high = index & (LANES - 1), index >> 7
         blocks = [halo.at[k, g].reshape(flat, LANES) for g in range(band_groups)]
         found = []
-
-        def select(r):
+        for r in rows:
             value = lookup(blocks[0][picked_rows(r), :], index_low)
             for g in range(1, band_groups):
                 value = jnp.where(
                     index_high == g, lookup(blocks[g][picked_rows(r), :], index_low), value
                 )
             found.append(value)
-
+        return found
+
+    def keep(at, start, rows, dense):
+        for r in range(0, len(rows), 2) if dense else ():
+            for part, item in enumerate(split(rows[r : r + 2])):
+                side[at, pl.ds((start + r) * SUB, 2 * SUB), cols(part)] = item
+        for r, item in enumerate(rows):
+            plain[at, pl.ds((start + r) * SUB, SUB), :] = item
+
+    def receive_rest(k, at, dense):
+        arrived(k, 0)
+        keep(at, mains + 2, rest_rows(select(k, range(mains, mains + line))), dense)
+
+    def receive_main(k, at):
+        found = []
         for h in range(halves):
+            arrived(k, 1 + h)
+            found += select(k, range(h * SUB, h * SUB + SUB))
+        keep(at, 0, main_rows(found), True)
+
+    for sem, filled in enumerate((fields, places, wanted)):
+        pltpu.make_async_copy(filled, filled, load_sem.at[sem]).wait()
+    pl.semaphore_wait(barrier, jnp.where(at_hub, n_all - 1, 2))
+    for k in (near, far):
+        ahead = k == 0
+        target = (jnp.where(ahead, right[0], left[0]), me_l)
+        start = jnp.where(ahead, groups - band_groups, 0)
+        for piece, where in enumerate(pieces()):
             for g in range(band_groups):
-                landed = halo.at[k, g, :, pl.ds(h * SUB, SUB), :]
-                pltpu.make_async_copy(landed, landed, halo_recv.at[k, g, h]).wait()
-            for r in range(h * SUB, h * SUB + SUB):
-                select(r)
-        for r in range(mains, mains + line):
-            select(r)
-        rows = as_rows(found[:mains], found[mains:])
-        for r in range(0, kinds, 2):
-            for part, item in enumerate(split(rows[r : r + 2])):
-                side[at, pl.ds(r * SUB, 2 * SUB), cols(part)] = item
-        for r, item in enumerate(rows):
-            plain[at, pl.ds(r * SUB, SUB), :] = item
-
-    for copy in loads:
-        copy.wait()
-    pl.semaphore_wait(barrier, jnp.where(at_hub, n_all - 1, 2))
-    sends = []
-    for k, (target, start) in enumerate(((right, e_dev - BAND), (left, 0))):
-        for h in range(halves):
-            for g in range(band_groups):
-                part = pl.ds(h * SUB, SUB)
-                send = pltpu.make_async_remote_copy(
-                    src_ref=natural.at[start // LANES + g, :, part, :],
-                    dst_ref=halo.at[k, g, :, part, :],
-                    send_sem=halo_send.at[k, g, h],
-                    recv_sem=halo_recv.at[k, g, h],
+                pltpu.make_async_remote_copy(
+                    src_ref=fields.at[(start + g, *where)],
+                    dst_ref=halo.at[(k, g, *where)],
+                    send_sem=halo_send,
+                    recv_sem=halo_recv.at[k, piece],
                     device_id=target,
                     device_id_type=MESH,
-                )
-                send.start()
-                sends.append(send)
+                ).start()
 
     @pl.when(at_hub)
     def _():
@@ -294,49 +307,57 @@
     prepare()
     zero = jnp.zeros((SUB, LANES), jnp.float32)
     sums = lax.fori_loop(
-        0, steps, functools.partial(gather_pass, own_found, spare, groups - 1, 0), (zero,) * 6, unroll=UNROLL
+        0, steps, functools.partial(gather_pass, own_found, spare, groups - 1, 0, (0, 1)), (zero,) * 6, unroll=UNROLL
     )
 
     lane = lax.broadcasted_iota(jnp.int32, (SUB, LANES), 1)
     row = lax.broadcasted_iota(jnp.int32, (SUB, LANES), 0)
     old_main = jnp.zeros((SUB, LANES), jnp.float32)
     for g in range(groups):
-        block = natural.at[g].reshape(flat, LANES)
+        block = fields.at[g].reshape((tracers + 4) * points, LANES)
         for j in range(mains):
-            old_main += block[picked_rows(j), :] * wide(masses_old[g, pl.ds(j, 1), :])
-    packed = jnp.where(lane == row, jnp.sum(old_main, axis=1, keepdims=True), 0.0)
+            old_main += block[picked_rows(j), :] * wide(fields[g, at_old, pl.ds(j, 1), :])
+    old_rest = jnp.zeros((SUB, LANES), jnp.float32)
     for t in range(SUB, tracers):
-        product = sum(natural[g, t] * masses_old[g] for g in range(groups))
-        total = jnp.sum(jnp.sum(product, axis=1, keepdims=True), axis=0, keepdims=True)
-        at = line * (t - SUB)
-        packed = jnp.where((lane == 4 * SUB + row) & (row == at), total, packed)
-
-    far = lax.rem(me_s, 2)
-    near = 1 - far
-    receive(near, 0)
+        product = sum(fields[g, t] * fields[g, at_old] for g in range(groups))
+        total = jnp.sum(product, axis=0, keepdims=True)
+        old_rest = jnp.where(row == line * (t - SUB), wide(total), old_rest)
+
+    receive_rest(near, 0, True)
+    receive_main(near, 0)
     sums = lax.fori_loop(
         0,
         steps,
-        functools.partial(gather_pass, functools.partial(near_found, near), plain.at[0], groups + near, 1),
+        functools.partial(gather_pass, functools.partial(near_found, near), plain.at[0], groups + near, 1, (0, 1)),
         sums,
         unroll=UNROLL,
     )
     lax.fori_loop(0, steps, functools.partial(foresee, far), 0, unroll=2)
-    receive(far, 1)
+    receive_rest(far, 1, False)
+    sums = lax.fori_loop(
+        0, steps, functools.partial(gather_pass, None, plain.at[1], groups + far, 2, (1,)), sums, unroll=UNROLL
+    )
+    receive_main(far, 1)
     sums = lax.fori_loop(
         0,
         steps,
-        functools.partial(gather_pass, far_found, plain.at[1], groups + far, 2),
+        functools.partial(gather_pass, far_found, plain.at[1], groups + far, 2, (0,)),
         sums,
         unroll=UNROLL,
     )
 
-    for b in range(2):
-        for q in range(3):
-            total = jnp.sum(sums[3 * b + q], axis=1, keepdims=True)
-            packed = jnp.where(lane == (4 * b + q + 1) * SUB + row, total, packed)
-    packed = jnp.sum(packed, axis=0, keepdims=True)
-    message[...] = packed
+    half = LANES // 2
+    deficit = room = jnp.zeros((SUB, LANES), jnp.float32)
+    for b, old in enumerate((old_main, old_rest)):
+        gap, up, down = [
+            jnp.sum(item, axis=1, keepdims=True) for item in (old - sums[3 * b], sums[3 * b + 1], sums[3 * b + 2])
+        ]
+        here, there = lane == b * SUB + row, lane == half + b * SUB + row
+        deficit = jnp.where(jnp.logical_or(here, there), gap, deficit)
+        room = jnp.where(here, up, jnp.where(there, down, room))
+    packed = [jnp.sum(item, axis=0, keepdims=True) for item in (deficit, room)]
+    for x in range(2):
+        message[pl.ds(x, 1), :] = packed[x]
 
     @pl.when(jnp.logical_not(at_hub))
     def _():
@@ -369,24 +390,27 @@
         return carry
 
     lax.fori_loop(0, points, arrange, 0, unroll=2)
-    for send in sends:
-        send.wait_send()
+    pltpu.make_async_copy(halo, halo, halo_send).wait()
     pltpu.make_async_copy(heard, heard, sum_recv).wait()
-    total = packed
-    for k in range(n_all - 1) if n_all <= 64 else ():
-        total = total + heard[k]
-    if n_all > 64:
-        total = lax.fori_loop(0, n_all - 1, lambda k, acc: acc + heard[k], total)
-
-    old, clip, up, down = [
-        wide(total) if q == 0 else pltpu.roll(wide(total), LANES - q * SUB, 1) for q in range(4)
-    ]
-    shortfall = old - clip
-    raised = jnp.where(shortfall >= 0, shortfall / up, 0.0)
-    lowered = jnp.where(shortfall >= 0, 0.0, shortfall / down)
+    totals = []
+    for x in range(2):
+        if n_all <= 64:
+            terms = [wide(packed[x])] + [wide(heard[k, pl.ds(x, 1), :]) for k in range(n_all - 1)]
+            while len(terms) > 1:
+                terms = [sum(terms[k : k + 2]) for k in range(0, len(terms), 2)]
+            totals.append(terms[0])
+        else:
+            totals.append(
+                lax.fori_loop(
+                    0, n_all - 1, lambda k, acc: acc + wide(heard[k, pl.ds(x, 1), :]), wide(packed[x])
+                )
+            )
+    shortfall, room = totals
+    raises = (shortfall >= 0) == (lane < half)
+    gain = jnp.where(raises, shortfall / room, 0.0)
     for b in range(2):
-        for x, gain in enumerate((raised, lowered)):
-            column = jnp.where(lane == 4 * b * SUB + row, gain, 0.0)
+        for x in range(2):
+            column = jnp.where(lane == half * x + b * SUB + row, gain, 0.0)
             gains[b, x] = jnp.broadcast_to(jnp.sum(column, axis=1, keepdims=True), (SUB, LANES))
     for t in range(tracers):
         b, at = (0, t) if t < SUB else (1, line * (t - SUB))
@@ -418,7 +442,7 @@
             in_specs=[pl.BlockSpec(memory_space=pl.ANY)] * 6,
             out_specs=vmem,
             scratch_shapes=[
-                pltpu.VMEM((groups, tracers, points, LANES), jnp.float32),
+                pltpu.VMEM((groups, tracers + 4, points, LANES), jnp.float32),
                 pltpu.VMEM((3, groups, rows, LANES), jnp.float32),
                 pltpu.VMEM(((groups - 1) * tall, 2 * LANES), jnp.bfloat16),
                 pltpu.VMEM((tall, LANES), jnp.float32),
@@ -428,17 +452,14 @@
                 pltpu.VMEM((points // 2, groups - 1, LANES, 2 * LANES), jnp.bfloat16),
                 pltpu.VMEM((groups, points * SUB, LANES), jnp.float32),
                 pltpu.VMEM((groups, points, LANES), jnp.int32),
-                pltpu.VMEM((groups, points, LANES), jnp.float32),
-                pltpu.VMEM((groups, points, LANES), jnp.float32),
-                pltpu.VMEM((groups, 2, points, LANES), jnp.float32),
                 pltpu.VMEM((2, cap), jnp.int32),
                 pltpu.VMEM((3, 2, 3, points, SUB, e_dev), jnp.float32),
                 pltpu.VMEM((2, 2, SUB, LANES), jnp.float32),
-                pltpu.VMEM((1, LANES), jnp.float32),
-                pltpu.VMEM((n_all - 1, 1, LANES), jnp.float32),
-                pltpu.SemaphoreType.DMA((5 * groups + 1,)),
-                pltpu.SemaphoreType.DMA((2, BAND // LANES, halves)),
-                pltpu.SemaphoreType.DMA((2, BAND // LANES, halves)),
+                pltpu.VMEM((2, LANES), jnp.float32),
+                pltpu.VMEM((n_all - 1, 2, LANES), jnp.float32),
+                pltpu.SemaphoreType.DMA((3,)),
+                pltpu.SemaphoreType.DMA,
+                pltpu.SemaphoreType.DMA((2, 1 + halves)),
                 pltpu.SemaphoreType.DMA,
                 pltpu.SemaphoreType.DMA,
                 pltpu.SemaphoreType.REGULAR,

time: 16.5 us -> 16.1 us (0.976)
  Pallas kernels: 15.6 us -> 15.2 us
    pallas_call x1, Pallas kernels: 15.6 us -> 15.2 us  [on_device(): pl.pallas_call(functools.partial(kernel, sizes), out_shape=pltpu.VMEM((ro...]
where the time goes in v3:
time: 16.1 us; the launch traced here: 15.9 us
  Pallas kernels  15.2 us (94%)
  local copies, waits for them, and re-layouts  0.7 us (4%)
    pallas_call x1, Pallas kernels, on_device(): pl.pallas_call(functools.partial(kernel, sizes), out_shape=pltpu.VMEM((ro...  15.2 us
    unnamed x1, local copies, waits for them, and re-layouts  0.7 us

profile of v3, /device:TPU:0, one launch (start us, length us, event | category | flops | bytes accessed | tf_op | source)
XLA Modules:
  0.0 15.9 jit_solution(7169993344901356905)
XLA Ops:
  0.0 15.2 %transport.1 = f32[160,384]{1,0:T(8,128)S(1)} custom-call(f32[10,16,384]{2,1,0:T(8,128)} %bitcast.8, f32[16,384]{1,0:T(8,128)} %bitcast.10, f32[16,384]{1,0:T(8,128)} %bitcast.11, f32[2,16,384]{2,1,0:T(8,128)} %bitcast.9, s32[16,384]{1,0:T(8,128)} %bitcast.12, s32[2,128]{1,0:T(2,128)} %bitcast.13), custom_call_target="tpu_custom_call" | custom-call | tf_op jit(solution)/shard_map/transport/pallas_call | solution.py:439
  15.2 0.7 %copy.8 = f32[1,10,16,384]{3,2,1,0:T(8,128)} copy(f32[1,10,16,384]{3,2,1,0:T(8,128)S(1)} %bitcast.7) | data formatting | bytes 491520

commit v4 on v3

--- a/solution.py
+++ b/solution.py
@@ -70,7 +70,7 @@
 
 def kernel(
     sizes, tr, air_old, air_new, coord, slot, fetch, out,
-    fields, stage, table, spare, halo, side, plain, picks, along, places, wanted,
+    fields, stage, table, spare, halo, side, plain, picks, along, lagrange, begun, places, wanted,
     kept, gains, message, heard, load_sem, halo_send, halo_recv, sum_send, sum_recv, ready,
 ):
     n_sfc, n_lev = sizes
@@ -84,7 +84,7 @@
     flat = tracers * points
     kinds = mains + line + 4
     tall = kinds * SUB
-    main_tall = (mains + 2) * SUB
+    half_rows = mains // 2
     band_groups = BAND // LANES
     steps = points // 2
     me_s, me_l = lax.axis_index("sfc"), lax.axis_index("lev")
@@ -158,6 +158,7 @@
                     table[at, cols(g % 2)] = item
         for g in range(groups):
             for i, term in enumerate(basis(fields[g, at_coord])):
+                lagrange[i, g] = term
                 for s in (i, i + line):
                     along[g, pl.ds(s, points, stride=SUB), :] = term
 
@@ -169,6 +170,19 @@
         rest = horner([point(mains + 2 + m) for m in range(line)], at_b)
         rest = folded(rest * along[e, pl.ds(n * SUB, SUB), :], jnp.add)
         return rest, point(mains + 2 + line), point(mains + 3 + line)
+
+    def half_sum(point, n, e, h):
+        at_b = wide(fields[e, at_coord + 1, pl.ds(n, 1), :])
+        pair = [
+            horner([point(line * x + m) for m in range(line)], at_b)
+            * wide(lagrange[2 * h + x, e, pl.ds(n, 1), :])
+            for x in range(2)
+        ]
+        return pair[0] + pair[1]
+
+    def end_sum(point, n, e, b):
+        value = begun[n, :, cols(e)] + half_sum(point, n, e, 1)
+        return value, point(half_rows), point(half_rows + 1)
 
     number = lax.broadcasted_iota(jnp.int32, (LANES, LANES), 0).astype(jnp.float32).astype(jnp.bfloat16)
 
@@ -198,16 +212,17 @@
         one = chosen(n, e, groups + k)
         return times(side[0], jnp.concatenate([one, one], axis=0))
 
-    def far_found(n, e):
+    def far_found(first, count, n, e):
         one = picks[n // 2, e]
-        return times(side[1, pl.ds(0, main_tall), :], jnp.concatenate([one, one], axis=0))
+        values = side[1, pl.ds(first * SUB, count * SUB), :]
+        return times(values, jnp.concatenate([one, one], axis=0))
 
     def foresee(k, i, carry):
         for e in range(groups - 1):
             picks[i, e] = chosen(2 * i, e, groups + k)
         return carry
 
-    def gather_pass(finder, values, group, turn, parts, i, carry):
+    def gather_pass(finder, values, group, turn, parts, blend, i, carry):
         sums = list(carry)
         n = 2 * i
         for e in range(groups):
@@ -228,7 +243,7 @@
 
                 mass = wide(fields[e, at_new, pl.ds(n + p, 1), :])
                 for b in parts:
-                    value, least, most = interpolate(point, n + p, e, b)
+                    value, least, most = blend(point, n + p, e, b)
                     clipped = jnp.minimum(jnp.maximum(value, least), most)
                     for q, kind in enumerate((clipped, most - clipped, clipped - least)):
                         if by_lookup:
@@ -237,14 +252,30 @@
                         kept[turn, b, q, n + p, :, cols(e)] = kind
         return tuple(sums)
 
+    def begin_pass(i, carry):
+        n = 2 * i
+        for e in range(groups):
+            found = None if e == groups - 1 else far_found(0, half_rows, n, e)
+            for p in range(2):
+                low_index = wide(places[e, pl.ds(n + p, 1), :]) & (LANES - 1)
+
+                def point(r):
+                    here = pl.ds(r * SUB, SUB)
+                    if found is None:
+                        return lookup(plain[1, here, :], low_index)
+                    return found[r * SUB : (r + 1) * SUB, p * LANES : (p + 1) * LANES]
+
+                begun[n + p, :, cols(e)] = half_sum(point, n + p, e, 0)
+        return carry
+
     def pieces():
         yield pl.ds(SUB, tracers - SUB), pl.ds(0, points)
         for h in range(halves):
             yield pl.ds(0, SUB), pl.ds(h * SUB, SUB)
 
     def arrived(k, piece):
-        landed = halo.at[(k, slice(None), *list(pieces())[piece])]
-        pltpu.make_async_copy(landed, landed, halo_recv.at[k, piece]).wait()
+        landed = halo.at[(k, slice(None), *list(pieces())[piece])] if piece <= halves else halo.at[k]
+        pltpu.make_async_copy(landed, landed, halo_recv.at[piece]).wait()
 
     def select(k, rows):
         index = wide(wanted[pl.ds(k, 1), :]) - jnp.where(k == 0, e_dev - BAND, 0)
@@ -268,33 +299,34 @@
             plain[at, pl.ds((start + r) * SUB, SUB), :] = item
 
     def receive_rest(k, at, dense):
-        arrived(k, 0)
         keep(at, mains + 2, rest_rows(select(k, range(mains, mains + line))), dense)
 
-    def receive_main(k, at):
-        found = []
-        for h in range(halves):
-            arrived(k, 1 + h)
-            found += select(k, range(h * SUB, h * SUB + SUB))
-        keep(at, 0, main_rows(found), True)
+    def receive_half(k, h, ranges):
+        arrived(k, 1 + h)
+        found = select(k, range(h * SUB, h * SUB + SUB))
+        ranges = [
+            functools.reduce(combine, found + before)
+            for combine, before in zip((jnp.minimum, jnp.maximum), ranges)
+        ]
+        rows = cubic(found[:line]) + cubic(found[line:])
+        keep(1, h * half_rows, rows + (ranges if h else []), True)
+        return [[item] for item in ranges]
 
     for sem, filled in enumerate((fields, places, wanted)):
         pltpu.make_async_copy(filled, filled, load_sem.at[sem]).wait()
     pl.semaphore_wait(barrier, jnp.where(at_hub, n_all - 1, 2))
     for k in (near, far):
         ahead = k == 0
-        target = (jnp.where(ahead, right[0], left[0]), me_l)
         start = jnp.where(ahead, groups - band_groups, 0)
-        for piece, where in enumerate(pieces()):
-            for g in range(band_groups):
-                pltpu.make_async_remote_copy(
-                    src_ref=fields.at[(start + g, *where)],
-                    dst_ref=halo.at[(k, g, *where)],
-                    send_sem=halo_send,
-                    recv_sem=halo_recv.at[k, piece],
-                    device_id=target,
-                    device_id_type=MESH,
-                ).start()
+        for piece, where in enumerate(pieces() if k is near else [(pl.ds(0, tracers), pl.ds(0, points))]):
+            pltpu.make_async_remote_copy(
+                src_ref=fields.at[(pl.ds(start, band_groups), *where)],
+                dst_ref=halo.at[(k, slice(None), *where)],
+                send_sem=halo_send,
+                recv_sem=halo_recv.at[piece if k is near else 1 + halves],
+                device_id=(jnp.where(ahead, right[0], left[0]), me_l),
+                device_id_type=MESH,
+            ).start()
 
     @pl.when(at_hub)
     def _():
@@ -307,7 +339,7 @@
     prepare()
     zero = jnp.zeros((SUB, LANES), jnp.float32)
     sums = lax.fori_loop(
-        0, steps, functools.partial(gather_pass, own_found, spare, groups - 1, 0, (0, 1)), (zero,) * 6, unroll=UNROLL
+        0, steps, functools.partial(gather_pass, own_found, spare, groups - 1, 0, (0, 1), interpolate), (zero,) * 6, unroll=UNROLL
     )
 
     lane = lax.broadcasted_iota(jnp.int32, (SUB, LANES), 1)
@@ -323,27 +355,29 @@
         total = jnp.sum(product, axis=0, keepdims=True)
         old_rest = jnp.where(row == line * (t - SUB), wide(total), old_rest)
 
+    arrived(near, 1 + halves)
     receive_rest(near, 0, True)
-    receive_main(near, 0)
+    keep(0, 0, main_rows(select(near, range(mains))), True)
     sums = lax.fori_loop(
         0,
         steps,
-        functools.partial(gather_pass, functools.partial(near_found, near), plain.at[0], groups + near, 1, (0, 1)),
+        functools.partial(gather_pass, functools.partial(near_found, near), plain.at[0], groups + near, 1, (0, 1), interpolate),
         sums,
         unroll=UNROLL,
     )
     lax.fori_loop(0, steps, functools.partial(foresee, far), 0, unroll=2)
+    arrived(far, 0)
     receive_rest(far, 1, False)
     sums = lax.fori_loop(
-        0, steps, functools.partial(gather_pass, None, plain.at[1], groups + far, 2, (1,)), sums, unroll=UNROLL
+        0, steps, functools.partial(gather_pass, None, plain.at[1], groups + far, 2, (1,), interpolate), sums, unroll=UNROLL
     )
-    receive_main(far, 1)
+    ranges = receive_half(far, 0, [[], []])
+    lax.fori_loop(0, steps, begin_pass, 0, unroll=UNROLL)
+    receive_half(far, 1, ranges)
+    finder = functools.partial(far_found, half_rows, half_rows + 2)
+    values = plain.at[1, pl.ds(half_rows * SUB, (half_rows + 2) * SUB), :]
     sums = lax.fori_loop(
-        0,
-        steps,
-        functools.partial(gather_pass, far_found, plain.at[1], groups + far, 2, (0,)),
-        sums,
-        unroll=UNROLL,
+        0, steps, functools.partial(gather_pass, finder, values, groups + far, 2, (0,), end_sum), sums, unroll=UNROLL
     )
 
     half = LANES // 2
@@ -431,10 +465,10 @@
         levels, tracers, points, e_dev = tracer_old.shape
         cap = fetch_list.shape[2]
         assert levels == 1 and cap == LANES and tracers == SUB + 2 and points == 16
-        assert e_dev // LANES % 2 == 1
+        assert e_dev // LANES % 2 == 1 and sizes[0] % 2 == 0
         rows = tracers * points
         groups, halves = e_dev // LANES, points // SUB
-        tall = (points + 8) * SUB
+        tall, line = (points + 8) * SUB, 4
         vmem = pl.BlockSpec(memory_space=pltpu.VMEM)
         result = pl.pallas_call(
             functools.partial(kernel, sizes),
@@ -451,6 +485,8 @@
                 pltpu.VMEM((2, tall, LANES), jnp.float32),
                 pltpu.VMEM((points // 2, groups - 1, LANES, 2 * LANES), jnp.bfloat16),
                 pltpu.VMEM((groups, points * SUB, LANES), jnp.float32),
+                pltpu.VMEM((line, groups, points, LANES), jnp.float32),
+                pltpu.VMEM((points, SUB, e_dev), jnp.float32),
                 pltpu.VMEM((groups, points, LANES), jnp.int32),
                 pltpu.VMEM((2, cap), jnp.int32),
                 pltpu.VMEM((3, 2, 3, points, SUB, e_dev), jnp.float32),
@@ -459,7 +495,7 @@
                 pltpu.VMEM((n_all - 1, 2, LANES), jnp.float32),
                 pltpu.SemaphoreType.DMA((3,)),
                 pltpu.SemaphoreType.DMA,
-                pltpu.SemaphoreType.DMA((2, 1 + halves)),
+                pltpu.SemaphoreType.DMA((2 + halves,)),
                 pltpu.SemaphoreType.DMA,
                 pltpu.SemaphoreType.DMA,
                 pltpu.SemaphoreType.REGULAR,

time: 16.1 us -> 16 us (level)
  no operation moved by 1% of the time
where the time goes in v4:
time: 16 us; the launch traced here: 15.8 us
  Pallas kernels  15.1 us (94%)
  local copies, waits for them, and re-layouts  0.7 us (4%)
    pallas_call x1, Pallas kernels, on_device(): pl.pallas_call(functools.partial(kernel, sizes), out_shape=pltpu.VMEM((ro...  15.1 us
    unnamed x1, local copies, waits for them, and re-layouts  0.7 us

profile of v4, /device:TPU:0, one launch (start us, length us, event | category | flops | bytes accessed | tf_op | source)
XLA Modules:
  0.0 15.8 jit_solution(7330726599924686475)
XLA Ops:
  0.0 15.1 %transport.1 = f32[160,384]{1,0:T(8,128)S(1)} custom-call(f32[10,16,384]{2,1,0:T(8,128)} %bitcast.8, f32[16,384]{1,0:T(8,128)} %bitcast.10, f32[16,384]{1,0:T(8,128)} %bitcast.11, f32[2,16,384]{2,1,0:T(8,128)} %bitcast.9, s32[16,384]{1,0:T(8,128)} %bitcast.12, s32[2,128]{1,0:T(2,128)} %bitcast.13), custom_call_target="tpu_custom_call" | custom-call | tf_op jit(solution)/shard_map/transport/pallas_call | solution.py:473
  15.1 0.7 %copy.8 = f32[1,10,16,384]{3,2,1,0:T(8,128)} copy(f32[1,10,16,384]{3,2,1,0:T(8,128)S(1)} %bitcast.7) | data formatting | bytes 491520

commit v5 on v4

--- a/solution.py
+++ b/solution.py
@@ -89,8 +89,8 @@
     steps = points // 2
     me_s, me_l = lax.axis_index("sfc"), lax.axis_index("lev")
     me = me_s * n_lev + me_l
-    right = (lax.rem(me_s + 1, n_sfc), me_l)
-    left = (lax.rem(me_s + n_sfc - 1, n_sfc), me_l)
+    right = (jnp.where(me_s == n_sfc - 1, 0, me_s + 1), me_l)
+    left = (jnp.where(me_s == 0, n_sfc - 1, me_s - 1), me_l)
     hub_s, hub_l = n_sfc - 1, n_lev - 1
     at_hub = me == n_all - 1
     far = lax.rem(me_s, 2)
@@ -371,7 +371,18 @@
     sums = lax.fori_loop(
         0, steps, functools.partial(gather_pass, None, plain.at[1], groups + far, 2, (1,), interpolate), sums, unroll=UNROLL
     )
+    half = LANES // 2
+
+    def add_masses(b, old, sums, deficit, room):
+        gap, up, down = [
+            jnp.sum(item, axis=1, keepdims=True) for item in (old - sums[3 * b], sums[3 * b + 1], sums[3 * b + 2])
+        ]
+        here, there = lane == b * SUB + row, lane == half + b * SUB + row
+        deficit = jnp.where(jnp.logical_or(here, there), gap, deficit)
+        return deficit, jnp.where(here, up, jnp.where(there, down, room))
+
     ranges = receive_half(far, 0, [[], []])
+    deficit, room = add_masses(1, old_rest, sums, zero, zero)
     lax.fori_loop(0, steps, begin_pass, 0, unroll=UNROLL)
     receive_half(far, 1, ranges)
     finder = functools.partial(far_found, half_rows, half_rows + 2)
@@ -380,15 +391,7 @@
         0, steps, functools.partial(gather_pass, finder, values, groups + far, 2, (0,), end_sum), sums, unroll=UNROLL
     )
 
-    half = LANES // 2
-    deficit = room = jnp.zeros((SUB, LANES), jnp.float32)
-    for b, old in enumerate((old_main, old_rest)):
-        gap, up, down = [
-            jnp.sum(item, axis=1, keepdims=True) for item in (old - sums[3 * b], sums[3 * b + 1], sums[3 * b + 2])
-        ]
-        here, there = lane == b * SUB + row, lane == half + b * SUB + row
-        deficit = jnp.where(jnp.logical_or(here, there), gap, deficit)
-        room = jnp.where(here, up, jnp.where(there, down, room))
+    deficit, room = add_masses(0, old_main, sums, deficit, room)
     packed = [jnp.sum(item, axis=0, keepdims=True) for item in (deficit, room)]
     for x in range(2):
         message[pl.ds(x, 1), :] = packed[x]

time: 16 us -> 15.9 us (level)
  no operation moved by 1% of the time
where the time goes in v5:
time: 15.9 us; the launch traced here: 15.8 us
  Pallas kernels  15.1 us (95%)
  local copies, waits for them, and re-layouts  0.7 us (4%)
    pallas_call x1, Pallas kernels, on_device(): pl.pallas_call(functools.partial(kernel, sizes), out_shape=pltpu.VMEM((ro...  15.1 us
    unnamed x1, local copies, waits for them, and re-layouts  0.7 us

profile of v5, /device:TPU:0, one launch (start us, length us, event | category | flops | bytes accessed | tf_op | source)
XLA Modules:
  0.0 15.8 jit_solution(12668063168450153714)
XLA Ops:
  0.0 15.1 %transport.1 = f32[160,384]{1,0:T(8,128)S(1)} custom-call(f32[10,16,384]{2,1,0:T(8,128)} %bitcast.8, f32[16,384]{1,0:T(8,128)} %bitcast.10, f32[16,384]{1,0:T(8,128)} %bitcast.11, f32[2,16,384]{2,1,0:T(8,128)} %bitcast.9, s32[16,384]{1,0:T(8,128)} %bitcast.12, s32[2,128]{1,0:T(2,128)} %bitcast.13), custom_call_target="tpu_custom_call" | custom-call | tf_op jit(solution)/shard_map/transport/pallas_call | solution.py:476
  15.1 0.7 %copy.8 = f32[1,10,16,384]{3,2,1,0:T(8,128)} copy(f32[1,10,16,384]{3,2,1,0:T(8,128)S(1)} %bitcast.7) | data formatting | bytes 491520
